TPU v7x, 32 devices: a whole 2x2x4 slice. The times are simulated.
32 devices in a mesh: dp: 4 (over y, x), land: 8 (over z, core).
Axes of the slice: x: 2, y: 2, z: 4, core: 2. Of those that a mesh axis runs over, the one named last changes fastest.
Arguments:
- items: bfloat16 [16384, 768], P(('dp', 'land')), may hold values from -1.5 to 1.5
- landmarks: bfloat16 [8192, 768], P('land'), may hold values from -1.5 to 1.5
- scales: float32 [8192], P('land'), may hold values from 0.25 to 1
- eigvecs: bfloat16 [8192, 256], P('land'), may hold values from -0.0625 to 0.0625
- eigvals: float32 [256], replicated, may hold values from 0.5 to 2
Outputs:
- coords: float32 [16384, 256], P(('dp', 'land'))
- gram: float32 [256, 256], replicated
All inputs are finite; a program needn't handle non-finite values.
Results may differ from a plain program's by a relative error of at most 0.0028.
Values may be sent and summed in bfloat16 or wider, within the bound.
No kernel may reach another device: no remote copies, remote signals or barrier semaphores. Data moves between devices by JAX's collectives and lax.ppermute only.
A program may use at most 128 MiB of HBM per device.

v0:
```python
import jax
import jax.numpy as jnp
from jax import lax
from jax.sharding import PartitionSpec as P


def kernel_block(rows, landmarks, scales):
    row_vals = rows.astype(jnp.float32)
    land_vals = landmarks.astype(jnp.float32)
    row_sq = jnp.sum(row_vals * row_vals, axis=1)
    land_sq = jnp.sum(land_vals * land_vals, axis=1)
    cross = jnp.dot(rows, landmarks.T, preferred_element_type=jnp.float32)
    dist = row_sq[:, None] + land_sq[None, :] - 2.0 * cross
    return jnp.exp(-dist * scales[None, :])


def per_device(items, landmarks, scales, eigvecs, eigvals):
    own_rows = items.shape[0]
    rows_all = own_rows * lax.axis_size("dp") * lax.axis_size("land")
    landmark_count = landmarks.shape[0] * lax.axis_size("land")
    kernel = kernel_block(lax.all_gather(items, "land", axis=0, tiled=True), landmarks, scales)
    land_degree = lax.psum(jnp.sum(kernel, axis=0), "dp")
    row_part = jnp.sum(kernel, axis=1)
    scaled = (kernel / jnp.sqrt(land_degree)[None, :]).astype(jnp.bfloat16)
    partial_value = jnp.dot(scaled, eigvecs, preferred_element_type=jnp.float32)
    summed, degrees = (
        lax.psum_scatter(partial_value, "land", scatter_dimension=0, tiled=True),
        lax.psum_scatter(row_part, "land", scatter_dimension=0, tiled=True),
    )
    factor = jnp.sqrt(jnp.float32(rows_all) * jnp.float32(landmark_count))
    coords = summed * (factor / jnp.sqrt(degrees))[:, None] / eigvals[None, :]
    outer = jnp.dot(coords.T, coords, precision=lax.Precision.HIGHEST)
    gram = lax.psum(outer, ("dp", "land")) / jnp.float32(rows_all)
    return (coords, gram)


def solution(mesh):
    return jax.shard_map(
        per_device,
        mesh=mesh,
        in_specs=(P(("dp", "land"), None), P("land", None), P("land"), P("land", None), P()),
        out_specs=(P(("dp", "land"), None), P()),
        check_vma=False,
    )
```

profile of v0, /device:TPU:0, one launch (start us, length us, event | category | flops | bytes accessed | tf_op | source)
XLA Modules:
  0.0 303.2 jit_solution(13520838185477166311)
XLA Ops:
  7.2 0.0 copy-start
  7.2 0.0 all-gather.2.cloned.1.call-start
  7.2 0.7 all-gather.2.cloned.1.call-update
  7.9 0.0 reduce-scatter.2.cloned.1.call-start
  8.0 1.8 multiply_reduce_fusion.1
  9.7 67.3 %all-gather.2.cloned.1.call-done = bf16[4096,768]{1,0:T(8,128)(2,1)} async-done(((bf16[512,768]{1,0:T(8,128)(2,1)}), bf16[4096,768]{1,0:T(8,128)(2,1)}) %all-gather.2.cloned.1.call-update) | async-done | bytes 6291472 | tf_op jit(solution)/shard_map/all_gather | solution.py:21
  77.1 4.1 %multiply_reduce_fusion = f32[4096]{0:T(1024)S(1)} fusion(bf16[4096,768]{1,0:T(8,128)(2,1)} %all-gather.2.cloned.1.call-done), kind=kLoop, calls=%fused_computation.2 | loop fusion | flops 9433088 | bytes 6307840 | tf_op jit(solution)/shard_map/reduce_sum | solution.py:10
  81.2 15.5 %fusion.2 = (f32[4096]{0:T(1024)S(1)}, f32[1024]{0:T(1024)S(1)}, f32[4096,1024]{1,0:T(8,128)}) fusion(f32[1024]{0:T(1024)} %param.7, bf16[4096,768]{1,0:T(8,128)(2,1)} %all-gather.2.cloned.1.call-done, bf16[1024,768]{1,0:T(8,128)(2,1)} %param.6, f32[1024]{0:T(1024)S(1)} %multiply_reduce_fusion.1, f32[4096]{0:T(1024)S(1)} %multiply_reduce_fusion), kind=kOutput, calls=%fused_computation.9 | convolution fusion | flops 6471805952 | bytes 24686592 | tf_op jit(solution)/shard_map/dot_general | solution.py:12
  96.6 9.8 %psum.14 = f32[1024]{0:T(1024)S(1)} all-reduce(f32[1024]{0:T(1024)S(1)} %get-tuple-element.3), channel_id=1, replica_groups=mesh['dp'=4,'land'=8] {'dp'}, use_global_device_ids=true, to_apply=%region_3.0 | all-reduce | flops 1024 | bytes 8192 | tf_op jit(solution)/shard_map/psum | solution.py:22
  106.5 0.0 copy-done
  106.5 0.0 copy-start.3
  106.5 0.0 copy-start.2
  106.5 10.1 %fusion = f32[4096,256]{1,0:T(8,128)} fusion(bf16[1024,256]{1,0:T(8,128)(2,1)S(1)} %copy-done, f32[4096,1024]{1,0:T(8,128)} %get-tuple-element.4, f32[1024]{0:T(1024)S(1)} %sqrt.6), kind=kOutput, calls=%fused_computation.3 | convolution fusion | flops 2155872256 | bytes 21499904 | tf_op jit(solution)/shard_map/dot_general | solution.py:25
  116.5 0.0 reduce-scatter.2.cloned.1.call-update
  116.6 0.0 all-reduce.3.cloned.1.call-start
  116.6 0.0 copy-done.3
  116.6 0.6 dynamic-slice
  117.9 27.3 %all-reduce = f32[4096]{0:T(1024)S(1)} all-reduce(f32[4096]{0:T(1024)S(1)} %get-tuple-element.2), channel_id=3, replica_groups=mesh['dp'=4,'land'=8] {'land'}, use_global_device_ids=true, to_apply=%region_6.0.clone | all-reduce | flops 4096 | bytes 32768
  145.1 0.1 fusion.1
  145.2 18.9 %reduce-scatter.2.cloned.1.call-done = f32[512,256]{1,0:T(8,128)} async-done(((f32[4096,256]{1,0:T(8,128)}), f32[512,256]{1,0:T(8,128)}) %reduce-scatter.2.cloned.1.call-update) | async-done | bytes 524304 | tf_op jit(solution)/shard_map/reduce_scatter | solution.py:27
  164.0 0.0 copy-done.2
  164.0 1.2 multiply_divide_fusion
  165.2 0.0 copy-start.1
  165.2 1.7 fusion.3
  167.0 0.0 all-reduce.3.cloned.1.call-update
  167.0 127.9 %all-reduce.3.cloned.1.call-done = f32[256,256]{1,0:T(8,128)} async-done(((f32[256,256]{1,0:T(8,128)}), f32[256,256]{1,0:T(8,128)}) %all-reduce.3.cloned.1.call-update) | async-done | bytes 262160 | tf_op jit(solution)/shard_map/psum | solution.py:33
  295.0 1.7 broadcast_multiply_fusion
  296.6 0.0 copy-done.1
  (1 shorter events, 0.0 us)
Async XLA Ops:
  7.2 99.3 %copy-start = (bf16[1024,256]{1,0:T(8,128)(2,1)S(1)}, bf16[1024,256]{1,0:T(8,128)(2,1)}, u32[]{:S(2)}) copy-start(bf16[1024,256]{1,0:T(8,128)(2,1)} %param.8) | copy-start | bytes 1572868
  7.2 69.9 %all-gather.2.cloned.1.call-start = ((), (), s32[]{:S(2)}) async-start(), calls=%async_computation.1 | async-start | bytes 7077888 | tf_op jit(solution)/shard_map/all_gather | solution.py:21
  7.9 156.1 %reduce-scatter.2.cloned.1.call-start = ((), (), s32[]{:S(2)}) async-start(), calls=%async_computation.2 | async-start | bytes 4718592 | tf_op jit(solution)/shard_map/reduce_scatter | solution.py:27
  106.5 10.2 %copy-start.3 = (u32[32]{0:T(128)S(1)}, u32[32]{0:T(128)}, u32[]{:S(2)}) copy-start(u32[32]{0:T(128)} %constant.11) | copy-start | bytes 388
  106.5 57.6 %copy-start.2 = (f32[256]{0:T(256)S(1)}, f32[256]{0:T(256)}, u32[]{:S(2)}) copy-start(f32[256]{0:T(256)} %param.9) | copy-start | bytes 3076
  116.6 178.4 %all-reduce.3.cloned.1.call-start = ((), (), s32[]{:S(2)}) async-start(), calls=%async_computation.3 | async-start | bytes 524288 | tf_op jit(solution)/shard_map/psum | solution.py:33
  165.2 131.4 %copy-start.1 = (f32[512,256]{1,0:T(8,128)}, f32[512,256]{1,0:T(8,128)S(1)}, u32[]{:S(2)}) copy-start(f32[512,256]{1,0:T(8,128)S(1)} %multiply_divide_fusion) | copy-start | bytes 1572868
Sparse Core Ops, SparseCore 0:
  9.6 67.4 all-gather.1
  116.7 47.3 reduce-scatter.1
  170.1 124.7 all-reduce.2
where the time goes:
time: 303 us
  waiting for transfers between devices  215 us (71%)
  blocking collectives  37.1 us (12%)
  matrix products  27.3 us (9%)
  between operations  14.5 us (5%)
  other arithmetic  8.79 us (3%)
    psum x1, waiting for transfers between devices, per_device(): gram = lax.psum(outer, ('dp', 'land')) / jnp.float32(rows_all)  128 us
    all_gather x1, waiting for transfers between devices, per_device(): lax.all_gather(items, 'land', axis=0, tiled=True)  67.3 us
    unnamed x1, blocking collectives  27.3 us
    reduce_scatter x1, waiting for transfers between devices, per_device(): lax.psum_scatter(partial_value, 'land', scatter_dimension=0, tiled=True)  18.9 us
    dot_general x1, matrix products, kernel_block(): cross = jnp.dot(rows, landmarks.T, preferred_element_type=jnp.float32)  15.5 us
    dot_general x1, matrix products, per_device(): partial_value = jnp.dot(scaled, eigvecs, preferred_element_type=jnp.float32)  10.1 us
    psum x1, blocking collectives, per_device(): land_degree = lax.psum(jnp.sum(kernel, axis=0), 'dp')  9.82 us
  transfers between devices with their start and end apart: 3, of which 3 were waited for; matrix products, arithmetic and copies ran while one was open for 1% of the time, Pallas kernels for 0%

commit v1 on v0

--- a/solution.py
+++ b/solution.py
@@ -2,6 +2,11 @@
 import jax.numpy as jnp
 from jax import lax
 from jax.sharding import PartitionSpec as P
+
+
+def gather_and_add(x, name):
+    blocks = lax.all_gather(x, name)
+    return jnp.sum(blocks, axis=0)
 
 
 def kernel_block(rows, landmarks, scales):
@@ -30,7 +35,7 @@
     factor = jnp.sqrt(jnp.float32(rows_all) * jnp.float32(landmark_count))
     coords = summed * (factor / jnp.sqrt(degrees))[:, None] / eigvals[None, :]
     outer = jnp.dot(coords.T, coords, precision=lax.Precision.HIGHEST)
-    gram = lax.psum(outer, ("dp", "land")) / jnp.float32(rows_all)
+    gram = gather_and_add(outer, ("dp", "land")) / jnp.float32(rows_all)
     return (coords, gram)
 
 

time: 303 us -> 254 us (0.84)
  waiting for transfers between devices: 215 us -> 163 us
    psum x1 -> x0, waiting for transfers between devices: 128 us -> none  [per_device(): gram = lax.psum(outer, ('dp', 'land')) / jnp.float32(rows_all)]
    all_gather x0 -> x1, waiting for transfers between devices: none -> 75.9 us  [gather_and_add(): blocks = lax.all_gather(x, name)]
    reduce_sum x0 -> x1, other arithmetic: none -> 3.94 us  [gather_and_add(): return jnp.sum(blocks, axis=0)]
where the time goes in v1:
time: 254 us
  waiting for transfers between devices  163 us (64%)
  blocking collectives  37.1 us (15%)
  matrix products  27.3 us (11%)
  between operations  14.5 us (6%)
  other arithmetic  11.8 us (5%)
    all_gather x1, waiting for transfers between devices, gather_and_add(): blocks = lax.all_gather(x, name)  75.9 us
    all_gather x1, waiting for transfers between devices, per_device(): lax.all_gather(items, 'land', axis=0, tiled=True)  67.3 us
    unnamed x1, blocking collectives  27.3 us
    reduce_scatter x1, waiting for transfers between devices, per_device(): lax.psum_scatter(partial_value, 'land', scatter_dimension=0, tiled=True)  18.9 us
    dot_general x1, matrix products, kernel_block(): cross = jnp.dot(rows, landmarks.T, preferred_element_type=jnp.float32)  15.5 us
    dot_general x1, matrix products, per_device(): partial_value = jnp.dot(scaled, eigvecs, preferred_element_type=jnp.float32)  10.1 us
    psum x1, blocking collectives, per_device(): land_degree = lax.psum(jnp.sum(kernel, axis=0), 'dp')  9.82 us
  transfers between devices with their start and end apart: 3, of which 3 were waited for; matrix products, arithmetic and copies ran while one was open for 1% of the time, Pallas kernels for 0%

profile of v1, /device:TPU:0, one launch (start us, length us, event | category | flops | bytes accessed | tf_op | source)
XLA Modules:
  0.0 254.1 jit_solution(10000682081972979356)
XLA Ops:
  7.2 0.0 copy-start
  7.2 0.0 all-gather.4.cloned.1.call-start
  7.2 0.7 all-gather.4.cloned.1.call-update
  7.9 0.0 reduce-scatter.2.cloned.1.call-start
  8.0 1.8 multiply_reduce_fusion.1
  9.7 67.3 %all-gather.4.cloned.1.call-done = bf16[4096,768]{1,0:T(8,128)(2,1)} async-done(((bf16[512,768]{1,0:T(8,128)(2,1)}), bf16[4096,768]{1,0:T(8,128)(2,1)}) %all-gather.4.cloned.1.call-update) | async-done | bytes 6291472 | tf_op jit(solution)/shard_map/all_gather | solution.py:26
  77.1 4.1 %multiply_reduce_fusion = f32[4096]{0:T(1024)S(1)} fusion(bf16[4096,768]{1,0:T(8,128)(2,1)} %all-gather.4.cloned.1.call-done), kind=kLoop, calls=%fused_computation.2 | loop fusion | flops 9433088 | bytes 6307840 | tf_op jit(solution)/shard_map/reduce_sum | solution.py:15
  81.2 15.5 %fusion.2 = (f32[4096]{0:T(1024)S(1)}, f32[1024]{0:T(1024)S(1)}, f32[4096,1024]{1,0:T(8,128)}) fusion(f32[1024]{0:T(1024)} %param.7, bf16[4096,768]{1,0:T(8,128)(2,1)} %all-gather.4.cloned.1.call-done, bf16[1024,768]{1,0:T(8,128)(2,1)} %param.6, f32[1024]{0:T(1024)S(1)} %multiply_reduce_fusion.1, f32[4096]{0:T(1024)S(1)} %multiply_reduce_fusion), kind=kOutput, calls=%fused_computation.9 | convolution fusion | flops 6471805952 | bytes 24686592 | tf_op jit(solution)/shard_map/dot_general | solution.py:17
  96.6 9.8 %psum.7 = f32[1024]{0:T(1024)S(1)} all-reduce(f32[1024]{0:T(1024)S(1)} %get-tuple-element.3), channel_id=1, replica_groups=mesh['dp'=4,'land'=8] {'dp'}, use_global_device_ids=true, to_apply=%region_3.0 | all-reduce | flops 1024 | bytes 8192 | tf_op jit(solution)/shard_map/psum | solution.py:27
  106.5 0.0 copy-done
  106.5 0.0 copy-start.3
  106.5 0.0 copy-start.2
  106.5 10.1 %fusion = f32[4096,256]{1,0:T(8,128)} fusion(bf16[1024,256]{1,0:T(8,128)(2,1)S(1)} %copy-done, f32[4096,1024]{1,0:T(8,128)} %get-tuple-element.4, f32[1024]{0:T(1024)S(1)} %sqrt.6), kind=kOutput, calls=%fused_computation.3 | convolution fusion | flops 2155872256 | bytes 21499904 | tf_op jit(solution)/shard_map/dot_general | solution.py:30
  116.5 0.0 reduce-scatter.2.cloned.1.call-update
  116.6 0.0 all-gather.6.cloned.1.call-start
  116.6 0.0 copy-done.3
  116.6 0.6 dynamic-slice
  117.9 27.3 %all-reduce = f32[4096]{0:T(1024)S(1)} all-reduce(f32[4096]{0:T(1024)S(1)} %get-tuple-element.2), channel_id=4, replica_groups=mesh['dp'=4,'land'=8] {'land'}, use_global_device_ids=true, to_apply=%region_6.0.clone | all-reduce | flops 4096 | bytes 32768
  145.1 0.1 fusion.1
  145.2 18.9 %reduce-scatter.2.cloned.1.call-done = f32[512,256]{1,0:T(8,128)} async-done(((f32[4096,256]{1,0:T(8,128)}), f32[512,256]{1,0:T(8,128)}) %reduce-scatter.2.cloned.1.call-update) | async-done | bytes 524304 | tf_op jit(solution)/shard_map/reduce_scatter | solution.py:32
  164.0 0.0 copy-done.2
  164.0 1.2 multiply_divide_fusion
  165.2 0.0 copy-start.1
  165.2 1.7 fusion.3
  167.0 0.0 all-gather.6.cloned.1.call-update
  167.0 75.9 %all-gather.6.cloned.1.call-done = f32[8192,256]{1,0:T(8,128)} async-done(((f32[256,256]{1,0:T(8,128)}), f32[8192,256]{1,0:T(8,128)}) %all-gather.6.cloned.1.call-update) | async-done | bytes 8388624 | tf_op jit(solution)/shard_map/all_gather | solution.py:8
  242.9 3.9 %reduce_sum.49 = f32[256,256]{1,0:T(8,128)S(1)} reduce(f32[32,256,256]{2,1,0:T(8,128)} %bitcast.7, f32[]{:T(128)} %constant.1.clone.1), dimensions={0}, to_apply=%region_7.0 | reduce | flops 2031616 | bytes 8650756 | tf_op jit(solution)/shard_map/reduce_sum | solution.py:9
  246.8 0.7 broadcast_multiply_fusion
  247.6 0.0 copy-done.1
  (1 shorter events, 0.0 us)
Async XLA Ops:
  7.2 99.3 %copy-start = (bf16[1024,256]{1,0:T(8,128)(2,1)S(1)}, bf16[1024,256]{1,0:T(8,128)(2,1)}, u32[]{:S(2)}) copy-start(bf16[1024,256]{1,0:T(8,128)(2,1)} %param.8) | copy-start | bytes 1572868
  7.2 69.9 %all-gather.4.cloned.1.call-start = ((), (), s32[]{:S(2)}) async-start(), calls=%async_computation.1 | async-start | bytes 7077888 | tf_op jit(solution)/shard_map/all_gather | solution.py:26
  7.9 156.1 %reduce-scatter.2.cloned.1.call-start = ((), (), s32[]{:S(2)}) async-start(), calls=%async_computation.2 | async-start | bytes 4718592 | tf_op jit(solution)/shard_map/reduce_scatter | solution.py:32
  106.5 10.2 %copy-start.3 = (u32[32]{0:T(128)S(1)}, u32[32]{0:T(128)}, u32[]{:S(2)}) copy-start(u32[32]{0:T(128)} %constant.11) | copy-start | bytes 388
  106.5 57.6 %copy-start.2 = (f32[256]{0:T(256)S(1)}, f32[256]{0:T(256)}, u32[]{:S(2)}) copy-start(f32[256]{0:T(256)} %param.9) | copy-start | bytes 3076
  116.6 126.3 %all-gather.6.cloned.1.call-start = ((), (), s32[]{:S(2)}) async-start(), calls=%async_computation.3 | async-start | bytes 8650752 | tf_op jit(solution)/shard_map/all_gather | solution.py:8
  165.2 82.3 %copy-start.1 = (f32[512,256]{1,0:T(8,128)}, f32[512,256]{1,0:T(8,128)S(1)}, u32[]{:S(2)}) copy-start(f32[512,256]{1,0:T(8,128)S(1)} %multiply_divide_fusion) | copy-start | bytes 1572868
Sparse Core Ops, SparseCore 0:
  9.6 67.4 all-gather.3
  116.7 47.3 reduce-scatter.1
  167.6 75.2 all-gather.5
